TPU v7x, 512 devices: a whole 4x4x16 slice. The times are simulated.
512 devices in a mesh: grp: 64 (over z, x_lo, core), tp: 8 (over x_hi, y).
Axes of the slice: x: 4 (x_hi: 2, x_lo: 2; x = x_hi * 2 + x_lo), y: 4, z: 16, core: 2. Of those that a mesh axis runs over, the one named last changes fastest.
Arguments:
- memory_rows: bfloat16 [65536, 4096], P('grp', 'tp'), may hold values from -24 to 24, as said below
- norm_gain: float32 [4096], replicated, may hold values from 0.25 to 1.75
- key_weight: bfloat16 [4096, 4096], P(None, 'tp'), may hold values from -0.09375 to 0.09375
- owner_table: int32 [8192], replicated, may hold values from 0 to 8191, as said below
Outputs:
- placed_keys: bfloat16 [65536, 4096], P('grp', 'tp')
Inputs may be any that keep to these rules, and one draw needn't show every extreme that they name: A permutation of the 8192 block numbers. Block b of the input goes to block position owner_table[b], which lies in group owner_table[b] // 128. The 128 blocks of one group go to all 64 groups, exactly 2 blocks to each of them. `memory_rows`: rows have offsets and scales of their own, and features a common pattern.
All inputs are finite; a program needn't handle non-finite values.
Results may differ from a plain program's by a relative error of at most 0.0049.
Values may be sent and summed in bfloat16 or wider, within the bound.
A program may use at most 64 MiB of HBM per device.

v0:
```python
import functools

import jax
import jax.numpy as jnp
from jax import lax
from jax.experimental import pallas as pl
from jax.experimental.pallas import tpu as pltpu
from jax.sharding import PartitionSpec as P

BLK_ROWS = 8
EPS = 1e-05
CHUNKS = 16
MIB = 1024 * 1024
MESH = pl.DeviceIdType.MESH


def flipped(me, mask, groups):
    out = me
    bit = 1
    while bit < groups:
        out = out + ((mask // bit) % 2) * bit * (1 - 2 * ((me // bit) % 2))
        bit *= 2
    return out


def mask_at(me, step, groups):
    quarter = groups // 4
    inner = ((me // quarter + 1) // 2) % 2
    turn = step // quarter
    first = (3 - turn) // 3
    second = (turn % 2) * (1 - turn // 2)
    third = (turn // 2) * (1 - turn % 2)
    far = first * (1 + inner) + 3 * second + third * (2 - inner)
    return far * quarter + quarter - 1 - step % quarter


def peer_mask(me, step, groups, early):
    regular = groups - early
    split = groups // 2 - early
    is_early = step // regular
    after = (1 + step // split) // 2
    late = step - regular + split
    return mask_at(me, is_early * late + (1 - is_early) * (step + early * after), groups)


def index_kernel(groups, per_chunk, table_ref, slot_ref, index_ref):
    me = lax.axis_index("grp")
    blocks = table_ref.shape[1]
    capacity = blocks // groups

    lane = lax.broadcasted_iota(jnp.int32, (groups, blocks), 1)
    row = lax.broadcasted_iota(jnp.int32, (groups, blocks), 0)
    peer = jnp.zeros((groups, blocks), jnp.int32)
    for step in range(groups):
        mask = peer_mask(me, step, groups, per_chunk)
        peer = jnp.where(row == step, flipped(me, mask, groups), peer)

    def ranked(offset, value):
        chosen = (offset >= 0) & (offset < blocks)
        counted = chosen.astype(jnp.int32)
        shift = 1
        while shift < blocks:
            counted = counted + jnp.where(lane >= shift, pltpu.roll(counted, shift, 1), 0)
            shift *= 2
        result = jnp.zeros((groups, blocks), jnp.int32)
        for r in range(capacity):
            at_rank = jnp.where(chosen & (counted == r + 1), value, 0).astype(jnp.float32)
            found = jnp.sum(at_rank, axis=1, keepdims=True).astype(jnp.int32)
            result = jnp.where(lane == r, found, result)
        return result

    own = jnp.broadcast_to(table_ref[pl.ds(me, 1), :], (groups, blocks))
    index_ref[...] = ranked(own - peer * blocks, lane)
    offset = table_ref[...] - me * blocks
    slot_ref[...] = ranked(offset, offset)


def place_kernel(groups, slot_ref, in_ref, out_ref, sem):
    me = lax.axis_index("grp")
    blocks = in_ref.shape[0]
    capacity = blocks // groups

    def move(i, carry):
        mask = i // capacity
        slot = slot_ref[me ^ mask, i - mask * capacity]
        pltpu.make_async_copy(in_ref.at[i], out_ref.at[slot], sem).start()
        return carry

    lax.fori_loop(0, blocks, move, 0, unroll=8)
    pltpu.make_async_copy(in_ref, out_ref, sem).wait()


def main_kernel(
    groups, parts, index_ref, rows_ref, gain_ref, weight_ref, out_ref,
    raw, away, mine, others, weight, keys, normed, gains,
    raw_sem, early_send, early_recv, weight_sem, gain_sem, gather_send, gather_recv, key_send, key_recv, self_sem,
):
    me = lax.axis_index("grp")
    part = lax.axis_index("tp")
    blocks, _, depth = rows_ref.shape
    row_count = blocks * BLK_ROWS
    width = depth * parts
    chunk = row_count // CHUNKS
    chunk_blocks = blocks // CHUNKS
    capacity = blocks // groups
    per_chunk = groups // CHUNKS
    piece = row_count // groups
    regular = groups - per_chunk

    barrier = pltpu.get_barrier_semaphore()
    def greet(i, carry):
        mask = groups - i
        pl.semaphore_signal(
            barrier, inc=1, device_id={"grp": flipped(me, mask, groups)}, device_id_type=MESH
        )
        return carry

    lax.fori_loop(1, groups, greet, 0)
    for j in range(1, parts):
        pl.semaphore_signal(
            barrier, inc=1, device_id={"tp": (part + j) % parts}, device_id_type=MESH
        )

    raw_copy = pltpu.make_async_copy(rows_ref, raw, raw_sem)

    def weight_copy(j):
        origin = (part + j) % parts
        return pltpu.make_async_copy(
            weight_ref.at[pl.ds(pl.multiple_of(origin * depth, depth), depth)],
            weight.at[pl.ds(j * depth, depth)],
            weight_sem.at[j],
        )

    def gain_copy(j):
        origin = (part + j) % parts
        return pltpu.make_async_copy(
            gain_ref.at[:, pl.ds(pl.multiple_of(origin * depth, depth), depth)],
            gains.at[:, pl.ds(j * depth, depth)],
            gain_sem.at[j],
        )

    def gather_copy(c, j):
        at = pl.ds(c * chunk_blocks, chunk_blocks)
        return pltpu.make_async_remote_copy(
            src_ref=mine.at[at],
            dst_ref=others.at[j - 1, at],
            send_sem=gather_send.at[j - 1, c],
            recv_sem=gather_recv.at[j - 1, c],
            device_id={"tp": (part + parts - j) % parts},
            device_id_type=MESH,
        )

    def key_copy(step):
        mask = peer_mask(me, step, groups, per_chunk)
        return pltpu.make_async_remote_copy(
            src_ref=keys.at[pl.ds(step * piece, piece)],
            dst_ref=out_ref.at[pl.ds(mask * piece, piece)],
            send_sem=key_send.at[step],
            recv_sem=key_recv.at[mask],
            device_id={"grp": flipped(me, mask, groups)},
            device_id_type=MESH,
        )

    def local_copy(i):
        step = regular + i if i < per_chunk else regular - 1
        mask = peer_mask(me, step, groups, per_chunk)
        return pltpu.make_async_copy(
            keys.at[pl.ds(step * piece, piece)],
            out_ref.at[pl.ds(mask * piece, piece)],
            self_sem.at[i],
        )

    def early_copy(i):
        mask = peer_mask(me, regular + i, groups, per_chunk)
        return pltpu.make_async_remote_copy(
            src_ref=away.at[pl.ds(i * capacity, capacity)],
            dst_ref=mine.at[pl.ds((regular + i) * capacity, capacity)],
            send_sem=early_send.at[i],
            recv_sem=early_recv.at[i],
            device_id={"grp": flipped(me, mask, groups)},
            device_id_type=MESH,
        )

    raw_copy.start()

    for j in range(parts):
        gain_copy(j).start()
    raw_copy.wait()
    for j in range(parts):
        weight_copy(j).start()

    def arrange(c):
        def take(i, carry):
            step = i // capacity
            block = raw[index_ref[step, i - step * capacity]]
            if c == CHUNKS - 1:
                away[i - c * chunk_blocks] = block
            else:
                mine[i] = block
            return carry

        lax.fori_loop(c * chunk_blocks, (c + 1) * chunk_blocks, take, 0, unroll=2)

    arrange(0)
    pl.semaphore_wait(barrier, groups - 1 + parts - 1)
    for c in range(CHUNKS - 1):
        if c > 0:
            arrange(c)
        for j in range(1, parts):
            gather_copy(c, j).start()
        if c == 0:
            arrange(CHUNKS - 1)
            for i in range(per_chunk):
                early_copy(i).start()
    for j in range(parts):
        gain_copy(j).wait()
        weight_copy(j).wait()

    sub = 2 * BLK_ROWS
    tile = depth

    def one_chunk(c, carry):
        base = pl.multiple_of(c * chunk, chunk)

        @pl.when(c == CHUNKS // 2)
        def _():
            for i in range(per_chunk):
                early_copy(i).wait_recv()
            for j in range(1, parts):
                gather_copy(CHUNKS - 1, j).start()

        for j in range(1, parts):
            gather_copy(c, j).wait_recv()

        def norm_rows(i, carry):
            at = pl.ds(c * chunk_blocks + i * 2, 2)
            to = pl.ds(pl.multiple_of(i * sub, sub), sub)

            def values(j):
                held = mine[at] if j == 0 else others[j - 1, at]
                return held.astype(jnp.float32).reshape(sub, depth)

            row_sum = 0.0
            row_sq = 0.0
            for j in range(parts):
                x = values(j)
                row_sum = row_sum + jnp.sum(x, axis=1, keepdims=True)
                row_sq = row_sq + jnp.sum(x * x, axis=1, keepdims=True)
            mean = row_sum / width
            scale = lax.rsqrt(row_sq / width - mean * mean + EPS)
            for j in range(parts):
                cols = pl.ds(j * depth, depth)
                normed[to, cols] = ((values(j) - mean) * scale * gains[:, cols]).astype(
                    jnp.bfloat16
                )
            return carry

        lax.fori_loop(0, chunk // sub, norm_rows, 0)

        def columns(n, carry):
            cols = pl.ds(pl.multiple_of(n * tile, tile), tile)
            keys[pl.ds(base, chunk), cols] = jnp.dot(
                normed[...], weight[:, cols], preferred_element_type=jnp.float32
            ).astype(jnp.bfloat16)
            return carry

        lax.fori_loop(0, keys.shape[1] // tile, columns, 0)

        for i in range(per_chunk):
            step = c * per_chunk + i

            @pl.when(step < regular - 1)
            def _():
                key_copy(step).start()

        @pl.when(c == CHUNKS - 2)
        def _():
            local_copy(per_chunk).start()

        return carry

    lax.fori_loop(0, CHUNKS, one_chunk, 0)

    for i in range(per_chunk):
        local_copy(i).start()
    for i in range(per_chunk):
        early_copy(i).wait_send()
    for c in range(CHUNKS):
        for j in range(1, parts):
            gather_copy(c, j).wait_send()

    def finish(step, carry):
        key_copy(step).wait()
        return carry

    lax.fori_loop(0, regular - 1, finish, 0)
    for i in range(per_chunk + 1):
        local_copy(i).wait()


def on_device(groups, parts, memory_rows, norm_gain, key_weight, owner_table):
    row_count, depth = memory_rows.shape
    columns = key_weight.shape[1]
    blocks = row_count // BLK_ROWS
    capacity = blocks // groups
    any_space = pl.BlockSpec(memory_space=pl.ANY)
    in_hbm = pl.BlockSpec(memory_space=pltpu.HBM)
    in_vmem = pl.BlockSpec(memory_space=pltpu.VMEM)
    in_smem = pl.BlockSpec(memory_space=pltpu.SMEM)

    dma = pltpu.SemaphoreType.DMA
    listing = jax.ShapeDtypeStruct((groups, blocks), jnp.int32)
    slots, index = pl.pallas_call(
        functools.partial(index_kernel, groups, groups // CHUNKS),
        out_shape=[listing, listing],
        in_specs=[in_vmem],
        out_specs=[in_vmem, in_vmem],
        compiler_params=pltpu.CompilerParams(vmem_limit_bytes=4 * MIB),
        name="index",
    )(owner_table.reshape(groups, blocks))

    incoming = pl.pallas_call(
        functools.partial(main_kernel, groups, parts),
        out_shape=jax.ShapeDtypeStruct((row_count, columns), jnp.bfloat16),
        in_specs=[in_smem, in_hbm, in_hbm, in_hbm],
        out_specs=any_space,
        scratch_shapes=[
            pltpu.VMEM((blocks, BLK_ROWS, depth), jnp.bfloat16),
            pltpu.VMEM((blocks // CHUNKS, BLK_ROWS, depth), jnp.bfloat16),
            pltpu.VMEM((blocks, BLK_ROWS, depth), jnp.bfloat16),
            pltpu.VMEM((parts - 1, blocks, BLK_ROWS, depth), jnp.bfloat16),
            pltpu.VMEM((depth * parts, columns), jnp.bfloat16),
            pltpu.VMEM((row_count, columns), jnp.bfloat16),
            pltpu.VMEM((row_count // CHUNKS, depth * parts), jnp.bfloat16),
            pltpu.VMEM((1, depth * parts), jnp.float32),
            dma,
            dma((groups // CHUNKS,)),
            dma((groups // CHUNKS,)),
            dma((parts,)),
            dma((parts,)),
            dma((parts - 1, CHUNKS)),
            dma((parts - 1, CHUNKS)),
            dma((groups,)),
            dma((groups,)),
            dma((groups // CHUNKS + 1,)),
        ],
        compiler_params=pltpu.CompilerParams(
            collective_id=0, has_side_effects=True, vmem_limit_bytes=48 * MIB
        ),
        name="exchange",
    )(index, memory_rows.reshape(blocks, BLK_ROWS, depth), norm_gain[None, :], key_weight)

    placed = pl.pallas_call(
        functools.partial(place_kernel, groups),
        out_shape=jax.ShapeDtypeStruct((blocks, BLK_ROWS, columns), jnp.bfloat16),
        in_specs=[in_smem, in_vmem],
        out_specs=any_space,
        scratch_shapes=[pltpu.SemaphoreType.DMA],
        compiler_params=pltpu.CompilerParams(vmem_limit_bytes=16 * MIB),
        name="place",
    )(slots, incoming.reshape(blocks, BLK_ROWS, columns))
    return placed.reshape(row_count, columns)


def solution(mesh):
    in_specs = (P("grp", "tp"), P(), P(None, "tp"), P())
    out_specs = P("grp", "tp")
    return jax.shard_map(
        functools.partial(on_device, mesh.shape["grp"], mesh.shape["tp"]),
        mesh=mesh, in_specs=in_specs, out_specs=out_specs, check_vma=False,
    )
```

profile of v0, /device:TPU:1, one launch (start us, length us, event | category | flops | bytes accessed | tf_op | source)
XLA Modules:
  0.0 141.1 jit_solution(13917034447104436690)
XLA Ops:
  0.0 0.0 copy-start.1
  0.0 0.8 copy-done.1
  0.8 1.5 %index.1 = (s32[64,128]{1,0:T(8,128)S(1)}, s32[64,128]{1,0:T(8,128)S(1)}) custom-call(s32[64,128]{1,0:T(8,128)S(1)} %bitcast.7), custom_call_target="tpu_custom_call" | custom-call | tf_op jit(solution)/shard_map/index/pallas_call | solution.py:313
  2.3 0.0 copy-start
  2.3 1.2 copy-done
  3.5 0.0 copy-start.2
  3.5 0.7 copy-done.2
  4.2 134.0 %exchange.1 = bf16[1024,512]{1,0:T(8,128)(2,1)S(1)} custom-call(s32[64,128]{1,0:T(8,128)S(1)} %get-tuple-element.8.index_ref, bf16[128,8,512]{2,1,0:T(8,128)(2,1)S(1)} %bitcast.6, f32[1,4096]{1,0:T(1,128)S(1)} %bitcast.8, bf16[4096,512]{1,0:T(8,128)(2,1)} %weight_ref.1), custom_call_target="tpu_custom_call" | custom-call | tf_op jit(solution)/shard_map/exchange/pallas_call | solution.py:322
  138.2 2.8 %place.1 = bf16[128,8,512]{2,1,0:T(8,128)(2,1)} custom-call(s32[64,128]{1,0:T(8,128)S(1)} %get-tuple-element.7.slot_ref, bf16[128,8,512]{2,1,0:T(8,128)(2,1)S(1)} %bitcast.5), custom_call_target="tpu_custom_call" | custom-call | tf_op jit(solution)/shard_map/place/pallas_call | solution.py:353
Async XLA Ops:
  0.0 0.8 copy-start.1
  2.3 1.2 copy-start
  3.5 0.7 copy-start.2
where the time goes:
time: 141 us
  Pallas kernels  138 us (98%)
  local copies, waits for them, and re-layouts  2.69 us (2%)
    pallas_call x1, Pallas kernels, on_device(): pl.pallas_call(functools.partial(main_kernel, groups, parts), out_shape=j...  134 us
    pallas_call x1, Pallas kernels, on_device(): pl.pallas_call(functools.partial(place_kernel, groups), out_shape=jax.Sha...  2.85 us

commit v1 on v0

v1 whole, which is shorter than its diff:
```python
import functools

import jax
import jax.numpy as jnp
from jax import lax
from jax.experimental import pallas as pl
from jax.experimental.pallas import tpu as pltpu
from jax.sharding import PartitionSpec as P

BLK_ROWS = 8
EPS = 1e-05
MIB = 1024 * 1024
MESH = pl.DeviceIdType.MESH

NZ = 16
NY = 4
NX = 4
PER_Z = 4
CHUNKS = 8
PIECES = 8
FIRST_OTHER = 5


def shift_of(i, e):
    odd = i % 2
    half = i // 2
    d = (1 - odd) * (half + 1) + odd * (7 - half) - 4 * (i // 7)
    return d + e * (NZ - 2 * d - 8 * (i // 7))


def core_served(x):
    return ((x + 1) // 2 + 1) % 2


def index_kernel(groups, table_ref, slot_ref, index_ref):
    me = lax.axis_index("grp")
    blocks = table_ref.shape[1]
    capacity = blocks // groups
    lane = lax.broadcasted_iota(jnp.int32, (groups, blocks), 1)
    row = lax.broadcasted_iota(jnp.int32, (groups, blocks), 0)

    def ranked(offset, value):
        chosen = (offset >= 0) & (offset < blocks)
        counted = chosen.astype(jnp.int32)
        shift = 1
        while shift < blocks:
            counted = counted + jnp.where(lane >= shift, pltpu.roll(counted, shift, 1), 0)
            shift *= 2
        result = jnp.zeros((groups, blocks), jnp.int32)
        for r in range(capacity):
            at_rank = jnp.where(chosen & (counted == r + 1), value, 0).astype(jnp.float32)
            found = jnp.sum(at_rank, axis=1, keepdims=True).astype(jnp.int32)
            result = jnp.where(lane == r, found, result)
        return result

    own = jnp.broadcast_to(table_ref[pl.ds(me, 1), :], (groups, blocks))
    index_ref[...] = ranked(own - row * blocks, lane)
    offset = table_ref[...] - me * blocks
    slot_ref[...] = ranked(offset, offset)


def place_kernel(slot_ref, in_ref, out_ref, sem):
    z = lax.axis_index("grp") // PER_Z
    blocks = in_ref.shape[0]

    def move(n, carry):
        s = n // (blocks // 2)
        i = (n // 8) % CHUNKS
        e = (n // 4) % 2
        a = (n // 2) % 2
        source = ((z - shift_of(i, e) + NZ) % NZ) * PER_Z + a * 2 + s
        slot = slot_ref[source, n % 2]
        pltpu.make_async_copy(in_ref.at[n], out_ref.at[slot], sem).start()
        return carry

    lax.fori_loop(0, blocks, move, 0, unroll=8)
    pltpu.make_async_copy(in_ref, out_ref, sem).wait()


def main_kernel(
    index_ref, rows_ref, gain_ref, weight_ref, out_ref,
    raw, away, gath, weight, other, keys, normed, gains,
    raw_sem, weight_sem, gain_sem, z_send, z_recv, y_send, y_recv, f_send, f_recv,
    b_send, b_recv, a_send, a_recv, c_send, c_recv, k_send, k_recv,
):
    g = lax.axis_index("grp")
    t = lax.axis_index("tp")
    z = g // PER_Z
    x_lo = (g // 2) % 2
    core = g % 2
    x_hi = t // NY
    y = t % NY
    x = x_lo + 2 * x_hi
    served = core_served(x)
    keeps = 1 - (served + core) % 2
    depth = rows_ref.shape[2]
    width = weight_ref.shape[0]
    parts = width // depth
    chunk = 8 * BLK_ROWS
    half = CHUNKS * chunk
    quarter = width // 4
    piece = quarter // PIECES

    a_peer = {"grp": g + 2 * (1 - 2 * x_lo), "tp": t}
    b_peer = {"grp": g + 2 * (1 - 2 * x_lo), "tp": t + NY * (1 - 2 * x_hi)}
    c_peer = {"grp": g + 1 - 2 * core, "tp": t}
    up = {"grp": g, "tp": x_hi * NY + (y + 1) % NY}
    down = {"grp": g, "tp": x_hi * NY + (y + NY - 1) % NY}

    barrier = pltpu.get_barrier_semaphore()
    for peer in (a_peer, b_peer, c_peer, up, down):
        pl.semaphore_signal(barrier, inc=1, device_id=peer, device_id_type=MESH)

    def greet(n, carry):
        zs = (z + n // NX) % NZ
        xs = (x + n) % NX

        @pl.when(n + 1 - keeps > 0)
        def _():
            pl.semaphore_signal(
                barrier, inc=1,
                device_id={"grp": zs * PER_Z + (xs % 2) * 2 + served, "tp": (xs // 2) * NY + y},
                device_id_type=MESH,
            )

        return carry

    lax.fori_loop(0, NZ * NX, greet, 0)

    raw_copy = pltpu.make_async_copy(rows_ref, raw, raw_sem)
    raw_copy.start()

    def origin(j):
        r, h = j // 2, j % 2
        return h * NY + (y + (0, NY - 1, 1, 2)[r]) % NY

    def weight_copy(j):
        return pltpu.make_async_copy(
            weight_ref.at[pl.ds(pl.multiple_of(origin(j) * depth, depth), depth)],
            weight.at[pl.ds(j * depth, depth)],
            weight_sem.at[j],
        )

    def gain_copy(j):
        return pltpu.make_async_copy(
            gain_ref.at[:, pl.ds(pl.multiple_of(origin(j) * depth, depth), depth)],
            gains.at[:, pl.ds(j * depth, depth)],
            gain_sem.at[j],
        )

    for j in range(parts):
        gain_copy(j).start()
    for j in range(parts):
        weight_copy(j).start()

    def self_step(i, n):
        e, xl, k = n // 4, (n // 2) % 2, n % 2
        differs = (xl + x_lo + 1) % 2 + (k + core) % 2
        return keeps * (i // (CHUNKS - 1)) * (1 - e) * (1 - (differs + 1) // 2)

    def self_source(i, m):
        h, e, a = m // 4, (m // 2) % 2, m % 2
        differs = (h + x_hi) % 2 + (a + x_lo) % 2
        return keeps * (i // (CHUNKS - 1)) * (1 - e) * (1 - (differs + 1) // 2)

    def z_copy(i, n):
        e, xl, k = n // 4, (n // 2) % 2, n % 2
        to_z = (z + shift_of(i, e)) % NZ
        c = (xl + 1 + 2 * core) % NX
        return pltpu.make_async_remote_copy(
            src_ref=away.at[i * 8 + n],
            dst_ref=gath.at[0, i, x_hi, pl.ds((e * 2 + x_lo) * 2, 2)],
            send_sem=z_send.at[i * 8 + n],
            recv_sem=z_recv.at[i * 8 + x_hi * 4 + e * 2 + x_lo],
            device_id={"grp": to_z * PER_Z + (c % 2) * 2 + k, "tp": (c // 2) * NY + y},
            device_id_type=MESH,
        )

    def z_arrival(i, m):
        h, e, a = m // 4, (m // 2) % 2, m % 2
        return pltpu.make_async_remote_copy(
            src_ref=away.at[i * 8 + m],
            dst_ref=gath.at[0, i, h, pl.ds((e * 2 + a) * 2, 2)],
            send_sem=z_send.at[i * 8 + m],
            recv_sem=z_recv.at[i * 8 + m],
            device_id=a_peer,
            device_id_type=MESH,
        )

    def y_copy(i, way):
        return pltpu.make_async_remote_copy(
            src_ref=gath.at[0, i],
            dst_ref=gath.at[1 + way, i],
            send_sem=y_send.at[way, i],
            recv_sem=y_recv.at[way, i],
            device_id=(up, down)[way],
            device_id_type=MESH,
        )

    def f_copy(i, way):
        return pltpu.make_async_remote_copy(
            src_ref=gath.at[1 + way, i, way],
            dst_ref=gath.at[3, i, way],
            send_sem=f_send.at[way, i],
            recv_sem=f_recv.at[way, i],
            device_id=(up, down)[way],
            device_id_type=MESH,
        )

    def piece_of(q, p):
        return pl.ds(pl.multiple_of(q * quarter + p * piece, piece), piece)

    def b_copy(p):
        at = piece_of((1 - x_lo) * 2 + core, p)
        return pltpu.make_async_remote_copy(
            src_ref=weight.at[at], dst_ref=other.at[at],
            send_sem=b_send.at[p], recv_sem=b_recv.at[p],
            device_id=b_peer, device_id_type=MESH,
        )

    def a_copy(p):
        at = piece_of(x_lo * 2 + core, p)
        return pltpu.make_async_remote_copy(
            src_ref=other.at[at], dst_ref=other.at[at],
            send_sem=a_send.at[p], recv_sem=a_recv.at[p],
            device_id=a_peer, device_id_type=MESH,
        )

    def c_copy(p, late):
        at = piece_of((x_lo + late * (1 - 2 * x_lo)) * 2 + core, p)
        return pltpu.make_async_remote_copy(
            src_ref=other.at[at], dst_ref=other.at[at],
            send_sem=c_send.at[late, p], recv_sem=c_recv.at[late, p],
            device_id=c_peer, device_id_type=MESH,
        )

    def rows_of(i):
        return pl.ds(pl.multiple_of(i * chunk, chunk), chunk)

    def k_copy(i, which):
        return pltpu.make_async_remote_copy(
            src_ref=keys.at[which, rows_of(i)],
            dst_ref=out_ref.at[pl.ds(pl.multiple_of(served * half + i * chunk, chunk), chunk)],
            send_sem=k_send.at[which, i],
            recv_sem=k_recv.at[which, i],
            device_id=(a_peer, b_peer)[which],
            device_id_type=MESH,
        )

    raw_copy.wait()

    def arrange(i):
        def take(n, carry):
            e, xl, k = n // 4, (n // 2) % 2, n % 2
            to = ((z + shift_of(i, e)) % NZ) * PER_Z + xl * 2 + k
            first = raw[index_ref[to, 0]]
            second = raw[index_ref[to, 1]]
            away[i * 8 + n, 0] = first
            away[i * 8 + n, 1] = second

            @pl.when(self_step(i, n) > 0)
            def _():
                gath[0, i, x_hi, (e * 2 + x_lo) * 2] = first
                gath[0, i, x_hi, (e * 2 + x_lo) * 2 + 1] = second

            return carry

        lax.fori_loop(0, 8, take, 0)

    def send_all(i, carry):
        def send(n, inner):
            @pl.when(self_step(i, n) < 1)
            def _():
                z_copy(i, n).start()

            return inner

        lax.fori_loop(0, 8, send, 0)
        return carry

    def arrange_all(i, carry):
        arrange(i)
        return carry

    lax.fori_loop(0, CHUNKS, arrange_all, 0)
    pl.semaphore_wait(barrier, NZ * NX - keeps + 5)
    lax.fori_loop(0, CHUNKS, send_all, 0)

    for j in range(parts):
        weight_copy(j).wait()
    for p in range(PIECES):
        b_copy(p).start()
    for j in range(parts):
        gain_copy(j).wait()

    sub = 2 * BLK_ROWS

    def normalise(i):
        def norm_rows(n, carry):
            to = pl.ds(pl.multiple_of(i * chunk + n * sub, sub), sub)

            def values(j):
                held = gath[j // 2, i, j % 2, pl.ds(n * 2, 2)]
                return held.astype(jnp.float32).reshape(sub, depth)

            row_sum = 0.0
            row_sq = 0.0
            for j in range(parts):
                v = values(j)
                row_sum = row_sum + jnp.sum(v, axis=1, keepdims=True)
                row_sq = row_sq + jnp.sum(v * v, axis=1, keepdims=True)
            mean = row_sum / width
            scale = lax.rsqrt(row_sq / width - mean * mean + EPS)
            for j in range(parts):
                cols = pl.ds(j * depth, depth)
                normed[to, cols] = ((values(j) - mean) * scale * gains[:, cols]).astype(
                    jnp.bfloat16
                )
            return carry

        lax.fori_loop(0, chunk // sub, norm_rows, 0)

    def project(i, which):
        keys[which, rows_of(i), :] = jnp.dot(
            normed[rows_of(i), :], (weight, other)[which][...],
            preferred_element_type=jnp.float32,
        ).astype(jnp.bfloat16)
        k_copy(i, which).start()

    def step(k, carry):
        @pl.when(k < CHUNKS)
        def _():
            def arrived(m, inner):
                @pl.when(self_source(k, m) < 1)
                def _():
                    z_arrival(k, m).wait_recv()

                return inner

            lax.fori_loop(0, 8, arrived, 0)
            for way in range(2):
                y_copy(k, way).start()

        @pl.when((k > 0) & (k <= CHUNKS))
        def _():
            for way in range(2):
                y_copy(k - 1, way).wait_recv()
                f_copy(k - 1, way).start()

        @pl.when(k < PIECES // 2)
        def _():
            for p in range(2):
                b_copy(k * 2 + p).wait_recv()
                a_copy(k * 2 + p).start()
                c_copy(k * 2 + p, 0).start()

        @pl.when((k > 0) & (k <= PIECES // 2))
        def _():
            for p in range(2):
                a_copy(k * 2 - 2 + p).wait_send()
                pltpu.make_async_remote_copy(
                    src_ref=other.at[piece_of(x_lo * 2 + core, k * 2 - 2 + p)],
                    dst_ref=other.at[piece_of((1 - x_lo) * 2 + core, k * 2 - 2 + p)],
                    send_sem=a_send.at[k * 2 - 2 + p], recv_sem=a_recv.at[k * 2 - 2 + p],
                    device_id=a_peer, device_id_type=MESH,
                ).wait_recv()
                c_copy(k * 2 - 2 + p, 1).start()

        @pl.when(k > 1)
        def _():
            for way in range(2):
                f_copy(k - 2, way).wait_recv()
            normalise(k - 2)
            project(k - 2, 0)

        @pl.when(k == FIRST_OTHER)
        def _():
            for p in range(PIECES):
                for late in range(2):
                    side = x_lo + late * (1 - 2 * x_lo)
                    pltpu.make_async_remote_copy(
                        src_ref=other.at[piece_of(side * 2 + core, p)],
                        dst_ref=other.at[piece_of(side * 2 + 1 - core, p)],
                        send_sem=c_send.at[late, p], recv_sem=c_recv.at[late, p],
                        device_id=c_peer, device_id_type=MESH,
                    ).wait_recv()

        @pl.when(k >= FIRST_OTHER)
        def _():
            def one(i, inner):
                project(i, 1)
                return inner

            start = (k - 2) * jnp.minimum(k - FIRST_OTHER, 1)
            lax.fori_loop(start, k - 1, one, 0)

        return carry

    lax.fori_loop(0, CHUNKS + 2, step, 0)

    def z_sent(n, carry):
        @pl.when(self_step(n // 8, n % 8) < 1)
        def _():
            z_copy(n // 8, n % 8).wait_send()

        return carry

    lax.fori_loop(0, CHUNKS * 8, z_sent, 0)

    def finish(i, carry):
        for way in range(2):
            y_copy(i, way).wait_send()
            f_copy(i, way).wait_send()
        for which in range(2):
            k_copy(i, which).wait_send()
            source = served + (1 - which) * (1 - 2 * served)
            pltpu.make_async_remote_copy(
                src_ref=keys.at[which, rows_of(i)],
                dst_ref=out_ref.at[pl.ds(pl.multiple_of(source * half + i * chunk, chunk), chunk)],
                send_sem=k_send.at[which, i], recv_sem=k_recv.at[which, i],
                device_id=(a_peer, b_peer)[which], device_id_type=MESH,
            ).wait_recv()
        return carry

    lax.fori_loop(0, CHUNKS, finish, 0)
    for p in range(PIECES):
        b_copy(p).wait_send()
        for late in range(2):
            c_copy(p, late).wait_send()


def on_device(groups, parts, memory_rows, norm_gain, key_weight, owner_table):
    row_count, depth = memory_rows.shape
    columns = key_weight.shape[1]
    blocks = row_count // BLK_ROWS
    any_space = pl.BlockSpec(memory_space=pl.ANY)
    in_hbm = pl.BlockSpec(memory_space=pltpu.HBM)
    in_vmem = pl.BlockSpec(memory_space=pltpu.VMEM)
    in_smem = pl.BlockSpec(memory_space=pltpu.SMEM)

    dma = pltpu.SemaphoreType.DMA
    listing = jax.ShapeDtypeStruct((groups, blocks), jnp.int32)
    slots, index = pl.pallas_call(
        functools.partial(index_kernel, groups),
        out_shape=[listing, listing],
        in_specs=[in_vmem],
        out_specs=[in_vmem, in_vmem],
        compiler_params=pltpu.CompilerParams(vmem_limit_bytes=4 * MIB),
        name="index",
    )(owner_table.reshape(groups, blocks))

    chunk_blocks = blocks // 2 // CHUNKS
    incoming = pl.pallas_call(
        main_kernel,
        out_shape=jax.ShapeDtypeStruct((row_count, columns), jnp.bfloat16),
        in_specs=[in_smem, in_hbm, in_hbm, in_hbm],
        out_specs=any_space,
        scratch_shapes=[
            pltpu.VMEM((blocks, BLK_ROWS, depth), jnp.bfloat16),
            pltpu.VMEM((blocks // 2, 2, BLK_ROWS, depth), jnp.bfloat16),
            pltpu.VMEM((NY, CHUNKS, 2, chunk_blocks, BLK_ROWS, depth), jnp.bfloat16),
            pltpu.VMEM((depth * parts, columns), jnp.bfloat16),
            pltpu.VMEM((depth * parts, columns), jnp.bfloat16),
            pltpu.VMEM((2, row_count // 2, columns), jnp.bfloat16),
            pltpu.VMEM((row_count // 2, depth * parts), jnp.bfloat16),
            pltpu.VMEM((1, depth * parts), jnp.float32),
            dma,
            dma((parts,)),
            dma((parts,)),
            dma((CHUNKS * 8,)),
            dma((CHUNKS * 8,)),
            dma((2, CHUNKS)),
            dma((2, CHUNKS)),
            dma((2, CHUNKS)),
            dma((2, CHUNKS)),
            dma((PIECES,)),
            dma((PIECES,)),
            dma((PIECES,)),
            dma((PIECES,)),
            dma((2, PIECES)),
            dma((2, PIECES)),
            dma((2, CHUNKS)),
            dma((2, CHUNKS)),
        ],
        compiler_params=pltpu.CompilerParams(
            collective_id=0, has_side_effects=True, vmem_limit_bytes=48 * MIB
        ),
        name="exchange",
    )(index, memory_rows.reshape(blocks, BLK_ROWS, depth), norm_gain[None, :], key_weight)

    placed = pl.pallas_call(
        place_kernel,
        out_shape=jax.ShapeDtypeStruct((blocks, BLK_ROWS, columns), jnp.bfloat16),
        in_specs=[in_smem, in_vmem],
        out_specs=any_space,
        scratch_shapes=[pltpu.SemaphoreType.DMA],
        compiler_params=pltpu.CompilerParams(vmem_limit_bytes=16 * MIB),
        name="place",
    )(slots, incoming.reshape(blocks, BLK_ROWS, columns))
    return placed.reshape(row_count, columns)


def solution(mesh):
    in_specs = (P("grp", "tp"), P(), P(None, "tp"), P())
    out_specs = P("grp", "tp")
    return jax.shard_map(
        functools.partial(on_device, mesh.shape["grp"], mesh.shape["tp"]),
        mesh=mesh, in_specs=in_specs, out_specs=out_specs, check_vma=False,
    )
```

time: 141 us -> 104 us (0.74)
  Pallas kernels: 138 us -> 101 us
    pallas_call x3, Pallas kernels: 138 us -> 101 us  [the longest x1 93.9 us: on_device(): pl.pallas_call(main_kernel, out_shape=jax.ShapeDtypeStruct((row_count, co...]
where the time goes in v1:
time: 104 us
  Pallas kernels  101 us (97%)
  local copies, waits for them, and re-layouts  2.69 us (3%)
    pallas_call x1, Pallas kernels, on_device(): pl.pallas_call(main_kernel, out_shape=jax.ShapeDtypeStruct((row_count, co...  93.9 us
    pallas_call x1, Pallas kernels, on_device(): pl.pallas_call(place_kernel, out_shape=jax.ShapeDtypeStruct((blocks, BLK_...  6.83 us
    unnamed x6, local copies, waits for them, and re-layouts  2.69 us

profile of v1, /device:TPU:1, one launch (start us, length us, event | category | flops | bytes accessed | tf_op | source)
XLA Modules:
  0.0 104.0 jit_solution(9538047620015776887)
XLA Ops:
  0.0 0.0 copy-start.1
  0.0 0.8 copy-done.1
  0.8 0.6 index.1
  1.4 0.0 copy-start
  1.4 1.2 %copy-done = bf16[1024,512]{1,0:T(8,128)(2,1)S(1)} copy-done((bf16[1024,512]{1,0:T(8,128)(2,1)S(1)}, bf16[1024,512]{1,0:T(8,128)(2,1)}, u32[]{:S(2)}) %copy-start) | copy-done | bytes 1048600
  2.6 0.0 copy-start.2
  2.6 0.7 copy-done.2
  3.3 93.9 %exchange.1 = bf16[1024,512]{1,0:T(8,128)(2,1)S(1)} custom-call(s32[64,128]{1,0:T(8,128)S(1)} %get-tuple-element.8.index_ref, bf16[128,8,512]{2,1,0:T(8,128)(2,1)S(1)} %bitcast.6, f32[1,4096]{1,0:T(1,128)S(1)} %bitcast.8, bf16[4096,512]{1,0:T(8,128)(2,1)} %weight_ref.1), custom_call_target="tpu_custom_call" | custom-call | tf_op jit(solution)/shard_map/exchange/pallas_call | solution.py:453
  97.2 6.8 %place.1 = bf16[128,8,512]{2,1,0:T(8,128)(2,1)} custom-call(s32[64,128]{1,0:T(8,128)S(1)} %get-tuple-element.7.slot_ref, bf16[128,8,512]{2,1,0:T(8,128)(2,1)S(1)} %bitcast.5), custom_call_target="tpu_custom_call" | custom-call | tf_op jit(solution)/shard_map/place/pallas_call | solution.py:491
Async XLA Ops:
  0.0 0.8 copy-start.1
  1.4 1.2 %copy-start = (bf16[1024,512]{1,0:T(8,128)(2,1)S(1)}, bf16[1024,512]{1,0:T(8,128)(2,1)}, u32[]{:S(2)}) copy-start(bf16[1024,512]{1,0:T(8,128)(2,1)} %param.4) | copy-start | bytes 3145732
  2.6 0.7 copy-start.2

commit v2 on v1

v2 whole, which is shorter than its diff:
```python
import functools

import jax
import jax.numpy as jnp
from jax import lax
from jax.experimental import pallas as pl
from jax.experimental.pallas import tpu as pltpu
from jax.sharding import PartitionSpec as P

BLK_ROWS = 8
EPS = 1e-05
MIB = 1024 * 1024
MESH = pl.DeviceIdType.MESH

NZ = 16
NY = 4
NX = 4
PER_Z = 4
SHIFTS = (3, 13, 4, 12, 5, 11, 1, 15, 7, 9, 2, 14, 6, 10, 8, 0)
STEPS = len(SHIFTS)
HOME_STEPS = 6
PIECES = 8
OTHER_CHUNK = 7
FIRST_HAND = (0, 0, 2, 3, 5, 6, 8, 10)
SECOND_HAND = (2, 2, 4, 5, 7, 8, 10, 12)
AHEAD = 2


def wrapped(v, n):
    return jnp.where(v >= n, v - n, v)


def core_served(x):
    return ((x + 1) // 2 + 1) % 2


def index_kernel(groups, table_ref, slot_ref, index_ref):
    me = lax.axis_index("grp")
    blocks = table_ref.shape[1]
    capacity = blocks // groups
    lane = lax.broadcasted_iota(jnp.int32, (groups, blocks), 1)
    row = lax.broadcasted_iota(jnp.int32, (groups, blocks), 0)

    def ranked(offset, value):
        chosen = (offset >= 0) & (offset < blocks)
        counted = chosen.astype(jnp.int32)
        shift = 1
        while shift < blocks:
            counted = counted + jnp.where(lane >= shift, pltpu.roll(counted, shift, 1), 0)
            shift *= 2
        result = jnp.zeros((groups, blocks), jnp.int32)
        for r in range(capacity):
            at_rank = jnp.where(chosen & (counted == r + 1), value, 0).astype(jnp.float32)
            found = jnp.sum(at_rank, axis=1, keepdims=True).astype(jnp.int32)
            result = jnp.where(lane == r, found, result)
        return result

    own = jnp.broadcast_to(table_ref[pl.ds(me, 1), :], (groups, blocks))
    index_ref[...] = ranked(own - row * blocks, lane)
    offset = table_ref[...] - me * blocks
    slot_ref[...] = ranked(offset, offset)


def place_kernel(slot_ref, in_ref, out_ref, sem):
    z = lax.axis_index("grp") // PER_Z
    for s in range(2):
        for j in range(STEPS):
            first = wrapped(z + (NZ - SHIFTS[j]) % NZ, NZ) * PER_Z + s
            for a in range(2):
                for r in range(2):
                    n = ((s * STEPS + j) * 2 + a) * 2 + r
                    slot = slot_ref[first + a * 2, r]
                    pltpu.make_async_copy(in_ref.at[n], out_ref.at[slot], sem).start()
    pltpu.make_async_copy(in_ref, out_ref, sem).wait()


def main_kernel(
    index_ref, rows_ref, gain_ref, weight_ref, out_ref,
    away, gath, weight, other, keys, normed, gains,
    weight_sem, s_send, s_recv, z_send, z_recv, y_send, y_recv, f_send, f_recv,
    b_send, b_recv, a_send, a_recv, c_send, c_recv, k_send, k_recv, h_send, h_recv,
):
    g = lax.axis_index("grp")
    t = lax.axis_index("tp")
    z = g // PER_Z
    x_lo = (g // 2) % 2
    core = g % 2
    x_hi = t // NY
    y = t % NY
    x = x_lo + 2 * x_hi
    served = core_served(x)
    keeps = 1 - (served + core) % 2
    depth = rows_ref.shape[2]
    width = weight_ref.shape[0]
    parts = width // depth
    sub = 2 * BLK_ROWS
    chunk = 4 * sub
    half = 2 * STEPS * sub
    chunks = half // chunk
    home_chunks = HOME_STEPS // 2
    quarter = width // 4
    piece = quarter // PIECES

    def at_device(z_at, x_at, core_at):
        high = jnp.where(x_at >= 2, 1, 0)
        return {"grp": z_at * PER_Z + (x_at - 2 * high) * 2 + core_at, "tp": high * NY + y}

    a_peer = at_device(z, x + 1 - 2 * x_lo, core)
    b_peer = at_device(z, NX - 1 - x, core)
    c_peer = at_device(z, x, 1 - core)
    y_up, y_down = wrapped(y + 1, NY), wrapped(y + NY - 1, NY)
    up = {"grp": g, "tp": x_hi * NY + y_up}
    down = {"grp": g, "tp": x_hi * NY + y_down}

    barrier = pltpu.get_barrier_semaphore()

    def signal(peer):
        pl.semaphore_signal(barrier, inc=1, device_id=peer, device_id_type=MESH)

    for peer in (a_peer, b_peer, c_peer, up, down):
        signal(peer)

    for j in range(HOME_STEPS, STEPS):
        zs = wrapped(z + (NZ - SHIFTS[j]) % NZ, NZ)
        for m in range(NX):
            if SHIFTS[j] == 0 and m == 0:
                @pl.when(keeps < 1)
                def _():
                    signal(at_device(zs, x, served))
            else:
                signal(at_device(zs, wrapped(x + m, NX), served))
    for j in range(HOME_STEPS):
        zs = wrapped(z + (NZ - SHIFTS[j]) % NZ, NZ)
        for m in range(4):
            signal(at_device(zs, wrapped(2 * core + 1 + m % 2, NX), m // 2))

    def origin(j):
        r, h = j // 2, j % 2
        return h * NY + (y, y_down, y_up, wrapped(y + 2, NY))[r]

    def weight_copy(j):
        return pltpu.make_async_copy(
            weight_ref.at[pl.ds(pl.multiple_of(origin(j) * depth, depth), depth)],
            weight.at[pl.ds(j * depth, depth)],
            weight_sem.at[j],
        )

    for j in range(parts):
        weight_copy(j).start()
    for j in range(parts):
        gains[:, pl.ds(j * depth, depth)] = gain_ref[
            :, pl.ds(pl.multiple_of(origin(j) * depth, depth), depth)
        ]

    mine = [
        keeps * jnp.where((x_hi == m // 2) & (x_lo == m % 2), 1, 0) for m in range(4)
    ]
    stays = [
        keeps * jnp.where((core == n // 2) & (x_lo == 1 - n % 2), 1, 0) for n in range(4)
    ]
    last = STEPS - 1

    def s_copy(j, which):
        k = which * served + (1 - which) * (1 - served)
        return pltpu.make_async_remote_copy(
            src_ref=away.at[pl.ds(j * 4 + k * 2, 2)],
            dst_ref=gath.at[0, j, x_hi],
            send_sem=s_send.at[which, j],
            recv_sem=s_recv.at[which, j],
            device_id=(a_peer, b_peer)[which],
            device_id_type=MESH,
        )

    def s_arrival(j, which):
        return pltpu.make_async_remote_copy(
            src_ref=away.at[pl.ds(j * 4, 2)],
            dst_ref=gath.at[0, j, x_hi + which * (1 - 2 * x_hi)],
            send_sem=s_send.at[which, j],
            recv_sem=s_recv.at[which, j],
            device_id=(a_peer, b_peer)[which],
            device_id_type=MESH,
        )

    def z_copy(j, n):
        return pltpu.make_async_remote_copy(
            src_ref=away.at[j * 4 + n],
            dst_ref=gath.at[0, j, x_hi, x_lo],
            send_sem=z_send.at[j * 4 + n],
            recv_sem=z_recv.at[j * 4 + x_hi * 2 + x_lo],
            device_id=at_device(
                wrapped(z + SHIFTS[j], NZ), wrapped(2 * core + n % 2 + 1, NX), n // 2
            ),
            device_id_type=MESH,
        )

    def z_arrival(j, m):
        return pltpu.make_async_remote_copy(
            src_ref=away.at[j * 4 + m],
            dst_ref=gath.at[0, j, m // 2, m % 2],
            send_sem=z_send.at[j * 4 + m],
            recv_sem=z_recv.at[j * 4 + m],
            device_id=a_peer,
            device_id_type=MESH,
        )

    def y_copy(j, way):
        return pltpu.make_async_remote_copy(
            src_ref=gath.at[0, j],
            dst_ref=gath.at[1 + way, j],
            send_sem=y_send.at[way, j],
            recv_sem=y_recv.at[way, j],
            device_id=(up, down)[way],
            device_id_type=MESH,
        )

    def f_copy(j, way):
        return pltpu.make_async_remote_copy(
            src_ref=gath.at[1 + way, j, way],
            dst_ref=gath.at[3, j, way],
            send_sem=f_send.at[way, j],
            recv_sem=f_recv.at[way, j],
            device_id=(up, down)[way],
            device_id_type=MESH,
        )

    def piece_of(q, p):
        return pl.ds(pl.multiple_of(q * quarter + p * piece, piece), piece)

    def b_copy(p):
        at = piece_of((1 - x_lo) * 2 + core, p)
        return pltpu.make_async_remote_copy(
            src_ref=weight.at[at], dst_ref=other.at[at],
            send_sem=b_send.at[p], recv_sem=b_recv.at[p],
            device_id=b_peer, device_id_type=MESH,
        )

    def b_arrival(p):
        at = piece_of(x_lo * 2 + core, p)
        return pltpu.make_async_remote_copy(
            src_ref=weight.at[at], dst_ref=other.at[at],
            send_sem=b_send.at[p], recv_sem=b_recv.at[p],
            device_id=b_peer, device_id_type=MESH,
        )

    def a_copy(p, side):
        at = piece_of((x_lo + side * (1 - 2 * x_lo)) * 2 + core, p)
        return pltpu.make_async_remote_copy(
            src_ref=other.at[at], dst_ref=other.at[at],
            send_sem=a_send.at[p], recv_sem=a_recv.at[p],
            device_id=a_peer, device_id_type=MESH,
        )

    def c_copy(p, late, at_core):
        at = piece_of((x_lo + late * (1 - 2 * x_lo)) * 2 + at_core, p)
        return pltpu.make_async_remote_copy(
            src_ref=other.at[at], dst_ref=other.at[at],
            send_sem=c_send.at[late, p], recv_sem=c_recv.at[late, p],
            device_id=c_peer, device_id_type=MESH,
        )

    def rows_of(i):
        return pl.ds(pl.multiple_of(i * chunk, chunk), chunk)

    def k_copy(i, which, source):
        return pltpu.make_async_remote_copy(
            src_ref=keys.at[which, rows_of(i)],
            dst_ref=out_ref.at[pl.ds(pl.multiple_of(source * half + i * chunk, chunk), chunk)],
            send_sem=k_send.at[which, i],
            recv_sem=k_recv.at[which, i],
            device_id=(a_peer, b_peer)[which],
            device_id_type=MESH,
        )

    def h_copy(n, which):
        side = x_hi + which * (1 - 2 * x_hi)
        at = (core * STEPS + n // 2) * 2 + 1 - x_lo
        return pltpu.make_async_remote_copy(
            src_ref=keys.at[which, pl.ds(pl.multiple_of(n * sub, sub), sub)],
            dst_ref=out_ref.at[pl.ds(pl.multiple_of(at * sub, sub), sub)],
            send_sem=h_send.at[which, n],
            recv_sem=h_recv.at[core, n // 2 * 2 + 1 - x_lo],
            device_id=at_device(wrapped(z + SHIFTS[n // 2], NZ), n % 2 + 2 * side, served),
            device_id_type=MESH,
        )

    def h_arrival(n, s):
        return pltpu.make_async_remote_copy(
            src_ref=keys.at[0, pl.ds(pl.multiple_of(n * sub, sub), sub)],
            dst_ref=out_ref.at[pl.ds(pl.multiple_of((s * STEPS * 2 + n) * sub, sub), sub)],
            send_sem=h_send.at[0, n],
            recv_sem=h_recv.at[s, n],
            device_id=a_peer,
            device_id_type=MESH,
        )

    def arrange(j):
        to_z = wrapped(z + SHIFTS[j], NZ) * PER_Z
        for n in range(4):
            to = to_z + (n % 2) * 2 + n // 2
            first = rows_ref[index_ref[to, 0]]
            second = rows_ref[index_ref[to, 1]]
            away[j * 4 + n, 0] = first
            away[j * 4 + n, 1] = second
            if j == last:
                @pl.when(stays[n] > 0)
                def _():
                    gath[0, j, x_hi, x_lo, 0] = first
                    gath[0, j, x_hi, x_lo, 1] = second

    for j in range(STEPS):
        arrange(j)
    pl.semaphore_wait(barrier, STEPS * 4 - keeps + 5)
    for j in range(HOME_STEPS):
        for which in range(2):
            s_copy(j, which).start()
    for j in range(HOME_STEPS, STEPS):
        for n in range(4):
            if j == last:
                @pl.when(stays[n] < 1)
                def _():
                    z_copy(j, n).start()
            else:
                z_copy(j, n).start()

    for j in range(parts):
        weight_copy(j).wait()
    for p in range(PIECES):
        b_copy(p).start()

    def normalise(i):
        def norm_rows(n, carry):
            to = pl.ds(pl.multiple_of(i * chunk + n * sub, sub), sub)

            def values(j):
                held = gath[j // 2, i * 2 + n // 2, j % 2, n - n // 2 * 2]
                return held.astype(jnp.float32).reshape(sub, depth)

            row_sum = 0.0
            row_sq = 0.0
            for j in range(parts):
                v = values(j)
                row_sum = row_sum + jnp.sum(v, axis=1, keepdims=True)
                row_sq = row_sq + jnp.sum(v * v, axis=1, keepdims=True)
            mean = row_sum / width
            scale = lax.rsqrt(row_sq / width - mean * mean + EPS)
            for j in range(parts):
                cols = pl.ds(j * depth, depth)
                normed[to, cols] = ((values(j) - mean) * scale * gains[:, cols]).astype(
                    jnp.bfloat16
                )
            return carry

        lax.fori_loop(0, chunk // sub, norm_rows, 0)

    def project(start, count, which):
        at = pl.ds(pl.multiple_of(start, chunk), count)
        keys[which, at, :] = jnp.dot(
            normed[at, :], (weight, other)[which][...], preferred_element_type=jnp.float32
        ).astype(jnp.bfloat16)

    def rows_arrived(i, e):
        for m in range(4):
            if e == last % 2:
                @pl.when((i < chunks - 1) | (mine[m] < 1))
                def _():
                    z_arrival(i * 2 + e, m).wait_recv()
            else:
                z_arrival(i * 2 + e, m).wait_recv()

    def forward(j):
        for way in range(2):
            y_copy(j, way).wait_recv()
            f_copy(j, way).start()

    def start_ring(j):
        for way in range(2):
            y_copy(j, way).start()

    def step(i, carry):
        for e in range(2):
            @pl.when(i < chunks)
            def _():
                forward(i * 2 + e)

            @pl.when((i + AHEAD >= home_chunks) & (i + AHEAD < chunks))
            def _():
                rows_arrived(i + AHEAD, e)
                start_ring((i + AHEAD) * 2 + e)

            for p in range(PIECES):
                if FIRST_HAND[p] % 2 == e:
                    @pl.when(i == FIRST_HAND[p] // 2)
                    def _():
                        b_arrival(p).wait_recv()
                        a_copy(p, 0).start()
                        c_copy(p, 0, core).start()

            for p in range(PIECES):
                if SECOND_HAND[p] % 2 == e:
                    @pl.when(i == SECOND_HAND[p] // 2)
                    def _():
                        a_copy(p, 1).wait_recv()
                        c_copy(p, 1, core).start()

        @pl.when(i > 0)
        def _():
            c = i - 1
            for e in range(2):
                for way in range(2):
                    f_copy(c * 2 + e, way).wait_recv()
            normalise(c)
            project(c * chunk, chunk, 0)

            for home in range(home_chunks):
                @pl.when(c == home)
                def _():
                    for n in range(home * 4, home * 4 + 4):
                        h_copy(n, 0).start()

            @pl.when(c >= home_chunks)
            def _():
                k_copy(c, 0, served).start()

        @pl.when(i == OTHER_CHUNK)
        def _():
            for p in range(PIECES):
                for late in range(2):
                    c_copy(p, late, 1 - core).wait_recv()
            project(0, home_chunks * chunk, 1)
            for n in range(home_chunks * 4):
                h_copy(n, 1).start()
            project(home_chunks * chunk, (OTHER_CHUNK - home_chunks) * chunk, 1)
            for c in range(home_chunks, OTHER_CHUNK):
                k_copy(c, 1, served).start()

        @pl.when(i > OTHER_CHUNK)
        def _():
            project((i - 1) * chunk, chunk, 1)
            k_copy(i - 1, 1, served).start()

        return carry

    for j in range(HOME_STEPS):
        for which in range(2):
            s_arrival(j, which).wait_recv()
        start_ring(j)
    lax.fori_loop(0, chunks + 1, step, 0)

    for j in range(HOME_STEPS, STEPS):
        for n in range(4):
            if j == last:
                @pl.when(stays[n] < 1)
                def _():
                    z_copy(j, n).wait_send()
            else:
                z_copy(j, n).wait_send()

    def home_sent(j, carry):
        for which in range(2):
            s_copy(j, which).wait_send()
        return carry

    def ring_sent(j, carry):
        for way in range(2):
            y_copy(j, way).wait_send()
            f_copy(j, way).wait_send()
        return carry

    def weight_sent(p, carry):
        b_copy(p).wait_send()
        a_copy(p, 0).wait_send()
        for late in range(2):
            c_copy(p, late, core).wait_send()
        return carry

    def keys_done(i, carry):
        for which in range(2):
            k_copy(i, which, served).wait_send()
            k_copy(i, which, served + (1 - which) * (1 - 2 * served)).wait_recv()
        return carry

    for n in range(HOME_STEPS * 2):
        for which in range(2):
            h_copy(n, which).wait_send()
            h_arrival(n, which).wait_recv()
    lax.fori_loop(0, HOME_STEPS, home_sent, 0)
    lax.fori_loop(0, STEPS, ring_sent, 0)
    lax.fori_loop(0, PIECES, weight_sent, 0)
    lax.fori_loop(home_chunks, chunks, keys_done, 0)


def on_device(groups, parts, memory_rows, norm_gain, key_weight, owner_table):
    row_count, depth = memory_rows.shape
    columns = key_weight.shape[1]
    blocks = row_count // BLK_ROWS
    any_space = pl.BlockSpec(memory_space=pl.ANY)
    in_hbm = pl.BlockSpec(memory_space=pltpu.HBM)
    in_vmem = pl.BlockSpec(memory_space=pltpu.VMEM)
    in_smem = pl.BlockSpec(memory_space=pltpu.SMEM)

    dma = pltpu.SemaphoreType.DMA
    listing = jax.ShapeDtypeStruct((groups, blocks), jnp.int32)
    slots, index = pl.pallas_call(
        functools.partial(index_kernel, groups),
        out_shape=[listing, listing],
        in_specs=[in_vmem],
        out_specs=[in_vmem, in_vmem],
        compiler_params=pltpu.CompilerParams(vmem_limit_bytes=4 * MIB),
        name="index",
    )(owner_table.reshape(groups, blocks))

    chunks = blocks // 16
    incoming = pl.pallas_call(
        main_kernel,
        out_shape=jax.ShapeDtypeStruct((row_count, columns), jnp.bfloat16),
        in_specs=[in_smem, in_vmem, in_vmem, in_hbm],
        out_specs=any_space,
        scratch_shapes=[
            pltpu.VMEM((STEPS * 4, 2, BLK_ROWS, depth), jnp.bfloat16),
            pltpu.VMEM((NY, STEPS, 2, 2, 2, BLK_ROWS, depth), jnp.bfloat16),
            pltpu.VMEM((depth * parts, columns), jnp.bfloat16),
            pltpu.VMEM((depth * parts, columns), jnp.bfloat16),
            pltpu.VMEM((2, row_count // 2, columns), jnp.bfloat16),
            pltpu.VMEM((row_count // 2, depth * parts), jnp.bfloat16),
            pltpu.VMEM((1, depth * parts), jnp.float32),
            dma((parts,)),
            dma((2, HOME_STEPS)),
            dma((2, HOME_STEPS)),
            dma((STEPS * 4,)),
            dma((STEPS * 4,)),
            dma((2, STEPS)),
            dma((2, STEPS)),
            dma((2, STEPS)),
            dma((2, STEPS)),
            dma((PIECES,)),
            dma((PIECES,)),
            dma((PIECES,)),
            dma((PIECES,)),
            dma((2, PIECES)),
            dma((2, PIECES)),
            dma((2, chunks)),
            dma((2, chunks)),
            dma((2, HOME_STEPS * 2)),
            dma((2, HOME_STEPS * 2)),
        ],
        compiler_params=pltpu.CompilerParams(
            collective_id=0, has_side_effects=True, vmem_limit_bytes=48 * MIB
        ),
        name="exchange",
    )(index, memory_rows.reshape(blocks, BLK_ROWS, depth), norm_gain[None, :], key_weight)

    placed = pl.pallas_call(
        place_kernel,
        out_shape=jax.ShapeDtypeStruct((blocks, BLK_ROWS, columns), jnp.bfloat16),
        in_specs=[in_smem, in_vmem],
        out_specs=any_space,
        scratch_shapes=[pltpu.SemaphoreType.DMA],
        compiler_params=pltpu.CompilerParams(vmem_limit_bytes=16 * MIB),
        name="place",
    )(slots, incoming.reshape(blocks, BLK_ROWS, columns))
    return placed.reshape(row_count, columns)


def solution(mesh):
    in_specs = (P("grp", "tp"), P(), P(None, "tp"), P())
    out_specs = P("grp", "tp")
    return jax.shard_map(
        functools.partial(on_device, mesh.shape["grp"], mesh.shape["tp"]),
        mesh=mesh, in_specs=in_specs, out_specs=out_specs, check_vma=False,
    )
```

time: 104 us -> 93.9 us (0.903)
  Pallas kernels: 101 us -> 90.9 us
    pallas_call x1, Pallas kernels: 93.9 us -> 88.1 us  [on_device(): pl.pallas_call(main_kernel, out_shape=jax.ShapeDtypeStruct((row_count, co...]
    pallas_call x1, Pallas kernels: 6.83 us -> 2.17 us  [on_device(): pl.pallas_call(place_kernel, out_shape=jax.ShapeDtypeStruct((blocks, BLK_...]
where the time goes in v2:
time: 93.9 us; the launch traced here: 93.6 us
  Pallas kernels  90.9 us (97%)
  local copies, waits for them, and re-layouts  2.69 us (3%)
    pallas_call x1, Pallas kernels, on_device(): pl.pallas_call(main_kernel, out_shape=jax.ShapeDtypeStruct((row_count, co...  88.1 us
    unnamed x6, local copies, waits for them, and re-layouts  2.69 us
    pallas_call x1, Pallas kernels, on_device(): pl.pallas_call(place_kernel, out_shape=jax.ShapeDtypeStruct((blocks, BLK_...  2.17 us

profile of v2, /device:TPU:1, one launch (start us, length us, event | category | flops | bytes accessed | tf_op | source)
XLA Modules:
  0.0 93.6 jit_solution(7000515711008869823)
XLA Ops:
  0.0 0.0 copy-start.1
  0.0 0.8 copy-done.1
  0.8 0.6 index.1
  1.4 0.0 copy-start
  1.4 1.2 %copy-done = bf16[1024,512]{1,0:T(8,128)(2,1)S(1)} copy-done((bf16[1024,512]{1,0:T(8,128)(2,1)S(1)}, bf16[1024,512]{1,0:T(8,128)(2,1)}, u32[]{:S(2)}) %copy-start) | copy-done | bytes 1048600
  2.6 0.0 copy-start.2
  2.6 0.7 copy-done.2
  3.3 88.1 %exchange.1 = bf16[1024,512]{1,0:T(8,128)(2,1)S(1)} custom-call(s32[64,128]{1,0:T(8,128)S(1)} %get-tuple-element.8.index_ref, bf16[128,8,512]{2,1,0:T(8,128)(2,1)S(1)} %bitcast.6, f32[1,4096]{1,0:T(1,128)S(1)} %bitcast.8, bf16[4096,512]{1,0:T(8,128)(2,1)} %weight_ref.1), custom_call_target="tpu_custom_call" | custom-call | tf_op jit(solution)/shard_map/exchange/pallas_call | solution.py:513
  91.4 2.2 %place.1 = bf16[128,8,512]{2,1,0:T(8,128)(2,1)} custom-call(s32[64,128]{1,0:T(8,128)S(1)} %get-tuple-element.7.slot_ref, bf16[128,8,512]{2,1,0:T(8,128)(2,1)S(1)} %bitcast.5), custom_call_target="tpu_custom_call" | custom-call | tf_op jit(solution)/shard_map/place/pallas_call | solution.py:552
Async XLA Ops:
  0.0 0.8 copy-start.1
  1.4 1.2 %copy-start = (bf16[1024,512]{1,0:T(8,128)(2,1)S(1)}, bf16[1024,512]{1,0:T(8,128)(2,1)}, u32[]{:S(2)}) copy-start(bf16[1024,512]{1,0:T(8,128)(2,1)} %param.4) | copy-start | bytes 3145732
  2.6 0.7 copy-start.2

commit v3 on v2

--- a/solution.py
+++ b/solution.py
@@ -16,13 +16,13 @@
 NY = 4
 NX = 4
 PER_Z = 4
-SHIFTS = (3, 13, 4, 12, 5, 11, 1, 15, 7, 9, 2, 14, 6, 10, 8, 0)
+SHIFTS = (3, 13, 4, 12, 5, 11, 1, 15, 2, 14, 6, 10, 7, 9, 8, 0)
 STEPS = len(SHIFTS)
 HOME_STEPS = 6
 PIECES = 8
 OTHER_CHUNK = 7
-FIRST_HAND = (0, 0, 2, 3, 5, 6, 8, 10)
-SECOND_HAND = (2, 2, 4, 5, 7, 8, 10, 12)
+FIRST_HAND = (1, 2, 3, 4, 6, 7, 8, 9)
+SECOND_HAND = (3, 4, 5, 6, 8, 9, 10, 12)
 AHEAD = 2
 
 
@@ -76,9 +76,10 @@
 
 def main_kernel(
     index_ref, rows_ref, gain_ref, weight_ref, out_ref,
-    away, gath, weight, other, keys, normed, gains,
-    weight_sem, s_send, s_recv, z_send, z_recv, y_send, y_recv, f_send, f_recv,
+    raw, away, gath, weight, other, keys, normed, gains,
+    raw_sem, weight_sem, gain_sem, s_send, s_recv, z_send, z_recv, y_send, y_recv, f_send, f_recv,
     b_send, b_recv, a_send, a_recv, c_send, c_recv, k_send, k_recv, h_send, h_recv,
+    token,
 ):
     g = lax.axis_index("grp")
     t = lax.axis_index("tp")
@@ -108,6 +109,9 @@
     a_peer = at_device(z, x + 1 - 2 * x_lo, core)
     b_peer = at_device(z, NX - 1 - x, core)
     c_peer = at_device(z, x, 1 - core)
+    raw_copy = pltpu.make_async_copy(rows_ref, raw, raw_sem)
+    raw_copy.start()
+
     y_up, y_down = wrapped(y + 1, NY), wrapped(y + NY - 1, NY)
     up = {"grp": g, "tp": x_hi * NY + y_up}
     down = {"grp": g, "tp": x_hi * NY + y_down}
@@ -117,22 +121,13 @@
     def signal(peer):
         pl.semaphore_signal(barrier, inc=1, device_id=peer, device_id_type=MESH)
 
-    for peer in (a_peer, b_peer, c_peer, up, down):
+    z_up = at_device(wrapped(z + 1, NZ), x, core)
+    z_down = at_device(wrapped(z + NZ - 1, NZ), x, core)
+    for peer in (up, down, z_up, z_down, c_peer):
         signal(peer)
-
-    for j in range(HOME_STEPS, STEPS):
-        zs = wrapped(z + (NZ - SHIFTS[j]) % NZ, NZ)
-        for m in range(NX):
-            if SHIFTS[j] == 0 and m == 0:
-                @pl.when(keeps < 1)
-                def _():
-                    signal(at_device(zs, x, served))
-            else:
-                signal(at_device(zs, wrapped(x + m, NX), served))
-    for j in range(HOME_STEPS):
-        zs = wrapped(z + (NZ - SHIFTS[j]) % NZ, NZ)
-        for m in range(4):
-            signal(at_device(zs, wrapped(2 * core + 1 + m % 2, NX), m // 2))
+    for m in range(1, NX):
+        for k in range(2):
+            signal(at_device(z, wrapped(x + m, NX), k))
 
     def origin(j):
         r, h = j // 2, j % 2
@@ -145,12 +140,17 @@
             weight_sem.at[j],
         )
 
+    def gain_copy(j):
+        return pltpu.make_async_copy(
+            gain_ref.at[:, pl.ds(pl.multiple_of(origin(j) * depth, depth), depth)],
+            gains.at[:, pl.ds(j * depth, depth)],
+            gain_sem.at[j],
+        )
+
     for j in range(parts):
         weight_copy(j).start()
     for j in range(parts):
-        gains[:, pl.ds(j * depth, depth)] = gain_ref[
-            :, pl.ds(pl.multiple_of(origin(j) * depth, depth), depth)
-        ]
+        gain_copy(j).start()
 
     mine = [
         keeps * jnp.where((x_hi == m // 2) & (x_lo == m % 2), 1, 0) for m in range(4)
@@ -297,8 +297,8 @@
         to_z = wrapped(z + SHIFTS[j], NZ) * PER_Z
         for n in range(4):
             to = to_z + (n % 2) * 2 + n // 2
-            first = rows_ref[index_ref[to, 0]]
-            second = rows_ref[index_ref[to, 1]]
+            first = raw[index_ref[to, 0]]
+            second = raw[index_ref[to, 1]]
             away[j * 4 + n, 0] = first
             away[j * 4 + n, 1] = second
             if j == last:
@@ -307,13 +307,16 @@
                     gath[0, j, x_hi, x_lo, 0] = first
                     gath[0, j, x_hi, x_lo, 1] = second
 
+    raw_copy.wait()
     for j in range(STEPS):
         arrange(j)
-    pl.semaphore_wait(barrier, STEPS * 4 - keeps + 5)
+    pl.semaphore_wait(barrier, 5 + 2 * (NX - 1))
     for j in range(HOME_STEPS):
         for which in range(2):
             s_copy(j, which).start()
-    for j in range(HOME_STEPS, STEPS):
+
+    def send_rows(shift):
+        j = SHIFTS.index(shift)
         for n in range(4):
             if j == last:
                 @pl.when(stays[n] < 1)
@@ -322,10 +325,44 @@
             else:
                 z_copy(j, n).start()
 
+    def start_ring(j):
+        for way in range(2):
+            y_copy(j, way).start()
+
+    def start_home(j):
+        for which in range(2):
+            s_arrival(j, which).wait_recv()
+        start_ring(j)
+
+    for d in range(1, NZ // 2 + 1):
+        ways = 2 if d < NZ // 2 else 1
+        for way in range(ways):
+            pl.semaphore_signal(
+                token.at[way, d - 1], inc=1, device_id=(z_up, z_down)[way], device_id_type=MESH
+            )
+        if d == 1:
+            send_rows(0)
+            for j in range(parts):
+                weight_copy(j).wait()
+            for p in range(PIECES):
+                b_copy(p).start()
+        for way in range(ways):
+            pl.semaphore_wait(token.at[way, d - 1], 1)
+        for shift in sorted({d, NZ - d}):
+            if shift in SHIFTS[HOME_STEPS:]:
+                send_rows(shift)
+        if d == 5:
+            start_home(0)
+            start_home(1)
+        if d == 7:
+            start_home(2)
+            start_home(3)
+    for j in range(4, HOME_STEPS):
+        start_home(j)
     for j in range(parts):
-        weight_copy(j).wait()
-    for p in range(PIECES):
-        b_copy(p).start()
+        gain_copy(j).wait()
+
+    sub = 2 * BLK_ROWS
 
     def normalise(i):
         def norm_rows(n, carry):
@@ -372,10 +409,6 @@
             y_copy(j, way).wait_recv()
             f_copy(j, way).start()
 
-    def start_ring(j):
-        for way in range(2):
-            y_copy(j, way).start()
-
     def step(i, carry):
         for e in range(2):
             @pl.when(i < chunks)
@@ -440,10 +473,6 @@
 
         return carry
 
-    for j in range(HOME_STEPS):
-        for which in range(2):
-            s_arrival(j, which).wait_recv()
-        start_ring(j)
     lax.fori_loop(0, chunks + 1, step, 0)
 
     for j in range(HOME_STEPS, STEPS):
@@ -513,9 +542,10 @@
     incoming = pl.pallas_call(
         main_kernel,
         out_shape=jax.ShapeDtypeStruct((row_count, columns), jnp.bfloat16),
-        in_specs=[in_smem, in_vmem, in_vmem, in_hbm],
+        in_specs=[in_smem, in_hbm, in_hbm, in_hbm],
         out_specs=any_space,
         scratch_shapes=[
+            pltpu.VMEM((blocks, BLK_ROWS, depth), jnp.bfloat16),
             pltpu.VMEM((STEPS * 4, 2, BLK_ROWS, depth), jnp.bfloat16),
             pltpu.VMEM((NY, STEPS, 2, 2, 2, BLK_ROWS, depth), jnp.bfloat16),
             pltpu.VMEM((depth * parts, columns), jnp.bfloat16),
@@ -523,6 +553,8 @@
             pltpu.VMEM((2, row_count // 2, columns), jnp.bfloat16),
             pltpu.VMEM((row_count // 2, depth * parts), jnp.bfloat16),
             pltpu.VMEM((1, depth * parts), jnp.float32),
+            dma,
+            dma((parts,)),
             dma((parts,)),
             dma((2, HOME_STEPS)),
             dma((2, HOME_STEPS)),
@@ -542,9 +574,10 @@
             dma((2, chunks)),
             dma((2, HOME_STEPS * 2)),
             dma((2, HOME_STEPS * 2)),
+            pltpu.SemaphoreType.REGULAR((2, NZ // 2)),
         ],
         compiler_params=pltpu.CompilerParams(
-            collective_id=0, has_side_effects=True, vmem_limit_bytes=48 * MIB
+            collective_id=0, has_side_effects=True, vmem_limit_bytes=52 * MIB
         ),
         name="exchange",
     )(index, memory_rows.reshape(blocks, BLK_ROWS, depth), norm_gain[None, :], key_weight)

time: 93.9 us -> 86.6 us (0.922)
  the two profiles are of different devices: /device:TPU:1 before, /device:TPU:2 now
where the time goes in v3:
time: 86.6 us; the launch traced here: 86.4 us
  Pallas kernels  84.9 us (98%)
  local copies, waits for them, and re-layouts  1.47 us (2%)
    pallas_call x1, Pallas kernels, on_device(): pl.pallas_call(main_kernel, out_shape=jax.ShapeDtypeStruct((row_count, co...  82.1 us
    pallas_call x1, Pallas kernels, on_device(): pl.pallas_call(place_kernel, out_shape=jax.ShapeDtypeStruct((blocks, BLK_...  2.17 us

profile of v3, /device:TPU:2, one launch (start us, length us, event | category | flops | bytes accessed | tf_op | source)
XLA Modules:
  0.0 86.4 jit_solution(1624777415961804533)
XLA Ops:
  0.0 0.0 copy-start
  0.0 0.8 copy-done
  0.8 0.6 index.1
  1.4 0.0 copy-start.1
  1.4 0.7 copy-done.1
  2.1 82.1 %exchange.1 = bf16[1024,512]{1,0:T(8,128)(2,1)S(1)} custom-call(s32[64,128]{1,0:T(8,128)S(1)} %get-tuple-element.8.index_ref, bf16[128,8,512]{2,1,0:T(8,128)(2,1)} %bitcast.8, f32[1,4096]{1,0:T(1,128)S(1)} %bitcast.7, bf16[4096,512]{1,0:T(8,128)(2,1)} %weight_ref.1), custom_call_target="tpu_custom_call" | custom-call | tf_op jit(solution)/shard_map/exchange/pallas_call | solution.py:542
  84.2 2.2 %place.1 = bf16[128,8,512]{2,1,0:T(8,128)(2,1)} custom-call(s32[64,128]{1,0:T(8,128)S(1)} %get-tuple-element.7.slot_ref, bf16[128,8,512]{2,1,0:T(8,128)(2,1)S(1)} %bitcast.5), custom_call_target="tpu_custom_call" | custom-call | tf_op jit(solution)/shard_map/place/pallas_call | solution.py:585
Async XLA Ops:
  0.0 0.8 copy-start
  1.4 0.7 copy-start.1

commit v4 on v3

--- a/solution.py
+++ b/solution.py
@@ -20,7 +20,7 @@
 STEPS = len(SHIFTS)
 HOME_STEPS = 6
 PIECES = 8
-OTHER_CHUNK = 7
+OTHER_CHUNK = 6
 FIRST_HAND = (1, 2, 3, 4, 6, 7, 8, 9)
 SECOND_HAND = (3, 4, 5, 6, 8, 9, 10, 12)
 AHEAD = 2

time: 86.6 us -> 84.2 us (0.972)
  the two profiles are of different devices: /device:TPU:2 before, /device:TPU:24 now
where the time goes in v4:
time: 84.2 us; the launch traced here: 84 us
  Pallas kernels  82.5 us (98%)
  local copies, waits for them, and re-layouts  1.47 us (2%)
    pallas_call x1, Pallas kernels, on_device(): pl.pallas_call(main_kernel, out_shape=jax.ShapeDtypeStruct((row_count, co...  79.7 us
    pallas_call x1, Pallas kernels, on_device(): pl.pallas_call(place_kernel, out_shape=jax.ShapeDtypeStruct((blocks, BLK_...  2.17 us

profile of v4, /device:TPU:24, one launch (start us, length us, event | category | flops | bytes accessed | tf_op | source)
XLA Modules:
  0.0 84.0 jit_solution(14202632372572587644)
XLA Ops:
  0.0 0.0 copy-start
  0.0 0.8 copy-done
  0.8 0.6 index.1
  1.4 0.0 copy-start.1
  1.4 0.7 copy-done.1
  2.1 79.7 %exchange.1 = bf16[1024,512]{1,0:T(8,128)(2,1)S(1)} custom-call(s32[64,128]{1,0:T(8,128)S(1)} %get-tuple-element.8.index_ref, bf16[128,8,512]{2,1,0:T(8,128)(2,1)} %bitcast.8, f32[1,4096]{1,0:T(1,128)S(1)} %bitcast.7, bf16[4096,512]{1,0:T(8,128)(2,1)} %weight_ref.1), custom_call_target="tpu_custom_call" | custom-call | tf_op jit(solution)/shard_map/exchange/pallas_call | solution.py:542
  81.8 2.2 %place.1 = bf16[128,8,512]{2,1,0:T(8,128)(2,1)} custom-call(s32[64,128]{1,0:T(8,128)S(1)} %get-tuple-element.7.slot_ref, bf16[128,8,512]{2,1,0:T(8,128)(2,1)S(1)} %bitcast.5), custom_call_target="tpu_custom_call" | custom-call | tf_op jit(solution)/shard_map/place/pallas_call | solution.py:585
Async XLA Ops:
  0.0 0.8 copy-start
  1.4 0.7 copy-start.1
